TPU v7x, 32 devices: a whole 2x2x4 slice. The times are simulated.
32 devices in a mesh: row: 4 (over x, core), col: 8 (over z, y).
Axes of the slice: x: 2, y: 2, z: 4, core: 2. Of those that a mesh axis runs over, the one named last changes fastest.
Arguments:
- matrix: float32 [2048, 8192], P('col', 'row'), may hold values from -6 to 6
- basis: float32 [8192, 512], P(('row', 'col')), may hold values from -0.0625 to 0.0625
Outputs:
- root: float32 [512, 512], P('row', 'col')
- right: float32 [2048, 512], P('col')
All inputs are finite; a program needn't handle non-finite values.
Results may differ from a plain program's by a relative error of at most 0.00018.
Values sent between devices are 32-bit elements; how exact they have to be, the bound alone decides.
A program may use at most 64 MiB of HBM per device.

v0:
```python
import functools

import jax
import jax.numpy as jnp
from jax import lax
from jax.experimental import pallas as pl
from jax.experimental.pallas import tpu as pltpu
from jax.sharding import PartitionSpec as P

ITERS = 8
OUTER = 4
CHUNKS = 2
LANES = 128
MESH = pl.DeviceIdType.MESH


def split(x):
    hi = x.astype(jnp.bfloat16)
    lo = (x - hi.astype(jnp.float32)).astype(jnp.bfloat16)
    return hi, lo


def dot3(a, b, dims=(((1,), (0,)), ((), ()))):
    dot = functools.partial(lax.dot_general, dimension_numbers=dims, preferred_element_type=jnp.float32)
    return dot(a[0], b[0]) + dot(a[0], b[1]) + dot(a[1], b[0])


def kernel(
    nrow, ncol, matrix, basis, root, right,
    slab, base, blocks, pieces, total, halves, parts, plane, partial, shares, gram, work,
    basis_send, basis_recv, piece_send, piece_recv, half_send, half_recv, part_send, part_recv,
    share_send, share_recv, line_send, line_recv,
    proj_send, proj_recv, mate_send, mate_recv,
    gram_send, gram_recv, twin_send, twin_recv, load,
):
    inner = ncol // OUTER
    nchip = nrow // 2 * inner
    row, col = lax.axis_index("row"), lax.axis_index("col")
    out, inn = col // inner, lax.rem(col, inner)
    core = lax.rem(row, 2)
    chip = row // 2 * inner + inn
    me = core * nchip + chip
    cols, depth, width = matrix.shape[0], basis.shape[0], basis.shape[1]
    high = plane.shape[0] // (2 * nchip)
    tall, wide = width // (2 * nchip), width // OUTER
    piece = depth // CHUNKS
    mate = {"row": row + 1 - 2 * core, "col": col}

    def chip_at(k):
        return lax.rem(chip + k, nchip)

    def chip_peer(k):
        other = chip_at(k)
        return {"row": other // inner * 2 + core, "col": out * inner + lax.rem(other, inner)}

    def line_peer(k):
        other = lax.rem(out + k, OUTER)
        return other, {"row": row, "col": other * inner + inn}

    def remote(src, dst, send, recv, device):
        return pltpu.make_async_remote_copy(
            src_ref=src, dst_ref=dst, send_sem=send, recv_sem=recv, device_id=device, device_id_type=MESH
        )

    loads = [pltpu.make_async_copy(basis, base, load.at[0]), pltpu.make_async_copy(matrix, slab, load.at[1])]
    for copy in loads:
        copy.start()
    barrier = pltpu.get_barrier_semaphore()
    greeted = [mate] + [chip_peer(k) for k in range(1, nchip)] + [line_peer(k)[1] for k in range(1, OUTER)]
    for device in greeted:
        pl.semaphore_signal(barrier, inc=1, device_id=device, device_id_type=MESH)
    pl.semaphore_wait(barrier, len(greeted))

    def block_copy(source, step, chunk, own=False):
        way = 0 if step > 0 else 1
        lines = pl.ds(chunk * piece, piece)
        here = blocks.at[source, lines, :]
        return remote(
            basis.at[lines, :] if own else here, here,
            basis_send.at[source, way, chunk], basis_recv.at[source, chunk],
            {"row": row, "col": (out + step) * inner + inn},
        )

    def both_ways(step):
        return out < OUTER - 1 if step > 0 else out > 0

    for step in (1, -1):
        @pl.when(both_ways(step))
        def _(step=step):
            for chunk in range(CHUNKS):
                block_copy(out, step, chunk, True).start()

    def piece_copy(k, at):
        other = lax.rem(inn + k, inner)
        device = {"row": row, "col": out * inner + other}
        start = pl.multiple_of((at * inner + other) * depth, depth)
        return remote(
            matrix.at[:, pl.ds(start, depth)], pieces.at[k - 1, at],
            piece_send.at[k - 1, at], piece_recv.at[k - 1, at], device,
        )

    for d in range(OUTER):
        for k in range(1, inner):
            piece_copy(k, lax.rem(out + d, OUTER)).start()

    def add_block(at, block, first=False):
        block_halves = split(block[...])
        for k in range(inner):
            if k == 0:
                start = pl.multiple_of((at * inner + inn) * depth, depth)
                mine = slab[:, pl.ds(start, depth)]
            else:
                piece_copy(k, at).wait_recv()
                mine = pieces[k - 1, at]
            home = pl.ds(pl.multiple_of(lax.rem(inn + inner - k, inner) * cols, cols), cols)
            got = dot3(split(mine), block_halves)
            total[home, :] = got if first else total[home, :] + got

    for copy in loads:
        copy.wait()
    add_block(out, base, True)
    for d in range(1, OUTER):
        for chunk in range(CHUNKS):
            for step in (1, -1):
                source = out - step * d

                @pl.when((source >= 0) & (source < OUTER))
                def _(source=source, step=step, chunk=chunk):
                    block_copy(source, step, chunk).wait_recv()

                    @pl.when(both_ways(step))
                    def _():
                        block_copy(source, step, chunk).start()

        for step in (1, -1):
            source = out - step * d

            @pl.when((source >= 0) & (source < OUTER))
            def _(source=source, step=step):
                add_block(source, blocks.at[source])

    def part(which, at):
        return pl.ds(pl.multiple_of((which * nchip + at) * high, high), high)

    order = list(range(1, nchip)) + [0]

    def half_copy(k):
        return remote(
            total.at[part(1 - core, chip_at(k)), :], halves.at[k], half_send.at[k], half_recv.at[k], mate
        )

    def part_copy(k):
        return remote(
            total.at[part(core, chip_at(k)), :], parts.at[k - 1], part_send.at[k - 1], part_recv.at[k - 1], chip_peer(k)
        )

    for k in order:
        half_copy(k).start()
    for at, k in enumerate(order):
        half_copy(k).wait_recv()
        spot = part(core, chip_at(k))
        total[spot, :] = total[spot, :] + halves[k]
        if at:
            part_copy(order[at - 1]).start()
    mine = total[part(core, chip), :]
    for k in range(1, nchip):
        part_copy(k).wait_recv()
        mine = mine + parts[k - 1]
    plane[part(core, chip), :] = mine

    def gather(buffer, size, send, recv, pair_send, pair_recv):
        def copy(which, at, send_sem, recv_sem, device):
            spot = buffer.at[pl.ds(pl.multiple_of((which * nchip + at) * size, size), size), :]
            return remote(spot, spot, send_sem, recv_sem, device)

        def from_chip(k):
            return lax.rem(chip + nchip - k, nchip)

        def away(k, at):
            return copy(core, at, send.at[k - 1], recv.at[k - 1], chip_peer(k))

        def across(k, which):
            return copy(which, from_chip(k), pair_send.at[k], pair_recv.at[k], mate)

        for k in range(1, nchip):
            away(k, chip).start()
        across(0, core).start()
        for k in range(1, nchip):
            away(k, from_chip(k)).wait_recv()
            across(k, core).start()
        for k in range(nchip):
            across(k, 1 - core).wait_recv()

        def finish():
            for k in range(1, nchip):
                away(k, chip).wait_send()
            for k in range(nchip):
                across(k, core).wait_send()

        return finish

    finish_proj = gather(plane, high, proj_send, proj_recv, mate_send, mate_recv)

    proj = split(plane[...])
    around = me * tall // LANES * LANES
    some = split(plane[:, pl.ds(pl.multiple_of(around, LANES), LANES)])
    partial[...] = dot3(some, proj, (((0,), (0,)), ((), ())))

    band = pl.ds(pl.multiple_of(me * tall, tall), tall)
    inside = pl.ds(pl.multiple_of(me * tall - around, tall), tall)

    def lanes(at):
        return pl.ds(pl.multiple_of(at * wide, wide), wide)

    shared = []
    for k in range(1, OUTER):
        other, device = line_peer(k)
        copy = remote(
            partial.at[inside, lanes(other)], shares.at[k - 1],
            share_send.at[k - 1], share_recv.at[k - 1], device,
        )
        copy.start()
        shared.append(copy)
    mine = partial[inside, lanes(out)]
    for k, copy in enumerate(shared):
        copy.wait_recv()
        mine = mine + shares[k]
    gram[band, lanes(out)] = mine

    def line_copy(k, at):
        spot = gram.at[band, lanes(at)]
        return remote(spot, spot, line_send.at[k - 1], line_recv.at[k - 1], line_peer(k)[1])

    for k in range(1, OUTER):
        line_copy(k, out).start()
    for k in range(1, OUTER):
        line_copy(k, lax.rem(out + OUTER - k, OUTER)).wait_recv()

    finish_gram = gather(gram, tall, gram_send, gram_recv, twin_send, twin_recv)

    whole = gram[...]
    scale = jnp.sqrt(jnp.sum(whole * whole, keepdims=True) + 1e-06)
    ident = (
        lax.broadcasted_iota(jnp.int32, (width, width), 0) == lax.broadcasted_iota(jnp.int32, (width, width), 1)
    ).astype(jnp.float32)
    root_scale = jnp.sqrt(scale)
    rows = root.shape[0]
    work[0:width, :] = whole / scale
    work[width : width + cols, :] = plane[pl.ds(pl.multiple_of(inn * cols, cols), cols), :]
    work[width + cols :, :] = gram[pl.ds(pl.multiple_of(col * rows, rows), rows), :] / scale

    def polar(step, carry):
        middle = split(1.5 * ident - 0.5 * work[0:width, :])
        got = dot3(split(work[...]), middle)
        work[width:, :] = got[width:, :]
        work[0:width, :] = dot3(split(got[:width, :]), middle)
        return carry

    lax.fori_loop(0, ITERS - 1, polar, 0)
    middle = split(1.5 * ident - 0.5 * work[0:width, :])
    got = dot3(split(work[width:, :]), middle)
    right[...] = got[:cols, :] / root_scale
    root[...] = got[cols:, :] * root_scale

    for step in (1, -1):
        @pl.when(both_ways(step))
        def _(step=step):
            for chunk in range(CHUNKS):
                block_copy(out, step, chunk, True).wait_send()
    for d in range(1, OUTER):
        for step in (1, -1):
            source = out - step * d

            @pl.when((source >= 0) & (source < OUTER) & both_ways(step))
            def _(source=source, step=step):
                for chunk in range(CHUNKS):
                    block_copy(source, step, chunk).wait_send()
    for d in range(OUTER):
        for k in range(1, inner):
            piece_copy(k, lax.rem(out + d, OUTER)).wait_send()
    for k in range(nchip):
        half_copy(k).wait_send()
    for k in range(1, nchip):
        part_copy(k).wait_send()
    for copy in shared:
        copy.wait_send()
    for k in range(1, OUTER):
        line_copy(k, out).wait_send()
    finish_proj()
    finish_gram()


def solution(mesh):
    nrow, ncol = mesh.shape["row"], mesh.shape["col"]
    inner = ncol // OUTER
    nchip = nrow // 2 * inner

    def local(matrix, basis):
        cols, (depth, width) = matrix.shape[0], basis.shape
        tall = inner * cols
        vmem = pl.BlockSpec(memory_space=pltpu.VMEM)

        def array(*shape):
            return pltpu.VMEM(shape, jnp.float32)

        def pair(*shape):
            return [pltpu.SemaphoreType.DMA(shape)] * 2

        root, right = pl.pallas_call(
            functools.partial(kernel, nrow, ncol),
            out_shape=(
                jax.ShapeDtypeStruct((width // ncol, width), jnp.float32),
                jax.ShapeDtypeStruct((cols, width), jnp.float32),
            ),
            in_specs=[pl.BlockSpec(memory_space=pltpu.HBM)] * 2,
            out_specs=(vmem, vmem),
            scratch_shapes=[
                array(*matrix.shape),
                array(depth, width),
                array(OUTER, depth, width),
                array(inner - 1, OUTER, cols, depth),
                array(tall, width),
                array(nchip, tall // (2 * nchip), width),
                array(nchip - 1, tall // (2 * nchip), width),
                array(tall, width),
                array(LANES, width),
                array(OUTER - 1, width // (2 * nchip), width // OUTER),
                array(width, width),
                array(width + cols + width // ncol, width),
                pltpu.SemaphoreType.DMA((OUTER, 2, CHUNKS)),
                pltpu.SemaphoreType.DMA((OUTER, CHUNKS)),
                *pair(inner - 1, OUTER),
                *pair(nchip),
                *pair(nchip - 1),
                *pair(OUTER - 1),
                *pair(OUTER - 1),
                *pair(nchip - 1),
                *pair(nchip),
                *pair(nchip - 1),
                *pair(nchip),
                pltpu.SemaphoreType.DMA((2,)),
            ],
            compiler_params=pltpu.CompilerParams(
                collective_id=0, has_side_effects=True, vmem_limit_bytes=40 * 1024 * 1024
            ),
        )(matrix, basis)
        long = width // nrow
        part = lax.dynamic_slice(root, (0, lax.axis_index("row") * long), (width // ncol, long))
        return part.T, right

    return jax.shard_map(
        local,
        mesh=mesh,
        in_specs=(P("col", "row"), P(("row", "col"), None)),
        out_specs=(P("row", "col"), P("col", None)),
        check_vma=False,
    )
```

profile of v0, /device:TPU:1, one launch (start us, length us, event | category | flops | bytes accessed | tf_op | source)
XLA Modules:
  0.0 100.8 jit_solution(8902371576047399403)
XLA Ops:
  0.6 0.0 copy-start
  0.6 1.6 %copy-done = f32[256,2048]{1,0:T(8,128)S(1)} copy-done((f32[256,2048]{1,0:T(8,128)S(1)}, f32[256,2048]{1,0:T(8,128)}, u32[]{:S(2)}) %copy-start) | copy-done | bytes 2097176
  2.2 0.0 copy-start.1
  2.2 1.0 %copy-done.1 = f32[256,512]{1,0:T(8,128)S(1)} copy-done((f32[256,512]{1,0:T(8,128)S(1)}, f32[256,512]{1,0:T(8,128)}, u32[]{:S(2)}) %copy-start.1) | copy-done | bytes 524312
  3.3 96.1 %shard_map.41 = (f32[64,512]{1,0:T(8,128)S(1)}, f32[256,512]{1,0:T(8,128)S(1)}) custom-call(f32[256,2048]{1,0:T(8,128)S(1)} %copy-done, f32[256,512]{1,0:T(8,128)S(1)} %copy-done.1), custom_call_target="tpu_custom_call" | custom-call | tf_op jit(solution)/shard_map/pallas_call | solution.py:309
  99.3 0.6 dynamic-slice_bitcast_fusion
  100.0 0.8 copy.5
Async XLA Ops:
  0.6 1.6 %copy-start = (f32[256,2048]{1,0:T(8,128)S(1)}, f32[256,2048]{1,0:T(8,128)}, u32[]{:S(2)}) copy-start(f32[256,2048]{1,0:T(8,128)} %matrix.1) | copy-start | bytes 6291460
  2.2 1.0 %copy-start.1 = (f32[256,512]{1,0:T(8,128)S(1)}, f32[256,512]{1,0:T(8,128)}, u32[]{:S(2)}) copy-start(f32[256,512]{1,0:T(8,128)} %basis.1) | copy-start | bytes 1572868
where the time goes:
time: 101 us
  Pallas kernels  96.1 us (95%)
  local copies, waits for them, and re-layouts  4.05 us (4%)
    pallas_call x1, Pallas kernels, local(): pl.pallas_call(functools.partial(kernel, nrow, ncol), out_shape=(jax.Shap...  96.1 us
    unnamed x5, local copies, waits for them, and re-layouts  3.42 us

commit v1 on v0

v1 whole, which is shorter than its diff:
```python
import functools

import jax
import jax.numpy as jnp
from jax import lax
from jax.experimental import pallas as pl
from jax.experimental.pallas import tpu as pltpu
from jax.sharding import PartitionSpec as P

ITERS = 8
OUTER = 4
LANES = 128
VMEM = 63 * 1024 * 1024
MESH = pl.DeviceIdType.MESH


def split(x):
    hi = x.astype(jnp.bfloat16)
    lo = (x - hi.astype(jnp.float32)).astype(jnp.bfloat16)
    return hi, lo


def dot3(a, b, dims=(((1,), (0,)), ((), ()))):
    dot = functools.partial(lax.dot_general, dimension_numbers=dims, preferred_element_type=jnp.float32)
    return dot(a[0], b[0]) + dot(a[0], b[1]) + dot(a[1], b[0])


def kernel(
    nrow, ncol, size, matrix, basis, root, right,
    slab, base, blocks, pieces, ahi, alo, total, halves, parts, plane, phi, plo, shares, gram, work,
    basis_send, basis_recv, piece_send, piece_recv, half_send, half_recv, part_send, part_recv,
    away_send, away_recv, mate_send, mate_recv, share_send, share_recv,
    gram_send, gram_recv, twin_send, twin_recv, load,
):
    inner = ncol // OUTER
    nchip = nrow // 2 * inner
    row, col = lax.axis_index("row"), lax.axis_index("col")
    out, inn = col // inner, lax.rem(col, inner)
    core = lax.rem(row, 2)
    chip = row // 2 * inner + inn
    me = core * nchip + chip
    cols, depth, width = matrix.shape[0], basis.shape[0], basis.shape[1]
    tall = plane.shape[0]
    high = tall // (2 * nchip)
    chunks = width // size
    thin = size // (2 * nchip)
    mate = {"row": row + 1 - 2 * core, "col": col}

    def chip_at(k):
        return lax.rem(chip + k, nchip)

    def from_chip(k):
        return lax.rem(chip + nchip - k, nchip)

    def chip_peer(k):
        other = chip_at(k)
        return {"row": other // inner * 2 + core, "col": out * inner + lax.rem(other, inner)}

    def line_peer(k):
        return {"row": row, "col": lax.rem(out + k, OUTER) * inner + inn}

    def remote(src, dst, send, recv, device):
        return pltpu.make_async_remote_copy(
            src_ref=src, dst_ref=dst, send_sem=send, recv_sem=recv, device_id=device, device_id_type=MESH
        )

    def lanes(c):
        return pl.ds(c * size, size)

    def own_columns(at):
        return pl.ds(pl.multiple_of((at * inner + inn) * depth, depth), depth)

    loads = [pltpu.make_async_copy(basis, base, load.at[OUTER])]
    loads += [pltpu.make_async_copy(matrix.at[:, own_columns(at)], slab.at[at], load.at[at]) for at in range(OUTER)]
    for copy in loads:
        copy.start()
    barrier = pltpu.get_barrier_semaphore()
    greeted = [mate] + [chip_peer(k) for k in range(1, nchip)] + [line_peer(k) for k in range(1, OUTER)]
    for device in greeted:
        pl.semaphore_signal(barrier, inc=1, device_id=device, device_id_type=MESH)
    pl.semaphore_wait(barrier, len(greeted))

    def block_copy(source, step, c, own=False):
        here = blocks.at[source, :, lanes(c)]
        return remote(
            basis.at[:, lanes(c)] if own else here, here,
            basis_send.at[source, 0 if step > 0 else 1, c], basis_recv.at[source, c],
            {"row": row, "col": (out + step) * inner + inn},
        )

    def both_ways(step):
        return out < OUTER - 1 if step > 0 else out > 0

    def inside(source):
        return (source >= 0) & (source < OUTER)

    for step in (1, -1):
        @pl.when(both_ways(step))
        def _(step=step):
            for c in range(chunks):
                block_copy(out, step, c, True).start()

    def piece_copy(k, at):
        other = lax.rem(inn + k, inner)
        device = {"row": row, "col": out * inner + other}
        start = pl.multiple_of((at * inner + other) * depth, depth)
        return remote(
            matrix.at[:, pl.ds(start, depth)], pieces.at[k - 1, at],
            piece_send.at[k - 1, at], piece_recv.at[k - 1, at], device,
        )

    for d in range(OUTER):
        for k in range(1, inner):
            piece_copy(k, lax.rem(out + d, OUTER)).start()

    def prepare(at, k):
        if k:
            piece_copy(k, at).wait_recv()
        home = pl.ds(pl.multiple_of(lax.rem(inn + inner - k, inner) * cols, cols), cols)
        ahi[at, home, :], alo[at, home, :] = split(pieces[k - 1, at] if k else slab[at])

    def add_block(at, block, where=slice(None), first=False):
        got = dot3((ahi[at], alo[at]), split(block[:, where]))
        total[:, where] = got if first else total[:, where] + got

    def pass_on(d, c):
        for step in (1, -1):
            source = out - step * d

            @pl.when(inside(source))
            def _(source=source, step=step):
                block_copy(source, step, c).wait_recv()

                @pl.when(both_ways(step))
                def _():
                    block_copy(source, step, c).start()

    for copy in loads:
        copy.wait()
    for at in range(OUTER):
        prepare(at, 0)
    for c in range(chunks):
        pass_on(1, c)
    for k in range(1, inner):
        prepare(out, k)
    add_block(out, base, first=True)
    for d in range(2, OUTER - 1):
        for c in range(chunks):
            pass_on(d, c)
    for d in range(1, OUTER):
        for k in range(1, inner):
            prepare(lax.rem(out + d, OUTER), k)
    for d in range(1, OUTER - 1):
        for step in (1, -1):
            source = out - step * d

            @pl.when(inside(source))
            def _(source=source):
                add_block(source, blocks.at[source])

    def half(which):
        return pl.ds(pl.multiple_of(which * nchip * high, nchip * high), nchip * high)

    def part(which, at):
        return pl.ds(pl.multiple_of((which * nchip + at) * high, high), high)

    def half_copy(c):
        return remote(total.at[half(1 - core), lanes(c)], halves.at[c], half_send.at[c], half_recv.at[c], mate)

    def part_copy(c, k):
        return remote(
            total.at[part(core, chip_at(k)), lanes(c)], parts.at[c, k - 1],
            part_send.at[c, k - 1], part_recv.at[c, k - 1], chip_peer(k),
        )

    def gather(spot_of, send, recv, pair_send, pair_recv):
        def copy(which, at, c, send_sem, recv_sem, device):
            spot = spot_of(which, at, c)
            return remote(spot, spot, send_sem, recv_sem, device)

        def away(c, k, at):
            return copy(core, at, c, send.at[c, k - 1], recv.at[c, k - 1], chip_peer(k))

        def across(c, k, which):
            return copy(which, from_chip(k), c, pair_send.at[c, k], pair_recv.at[c, k], mate)

        def begin(c):
            for k in range(1, nchip):
                away(c, k, chip).start()
            across(c, 0, core).start()

        def relay(c):
            for k in range(1, nchip):
                away(c, k, from_chip(k)).wait_recv()
                across(c, k, core).start()

        def end(c):
            for k in range(nchip):
                across(c, k, 1 - core).wait_recv()

        def finish(c):
            for k in range(1, nchip):
                away(c, k, chip).wait_send()
            for k in range(nchip):
                across(c, k, core).wait_send()

        return begin, relay, end, finish

    def slim(which, at, c):
        return pl.ds(pl.multiple_of(c * size + (which * nchip + at) * thin, thin), thin)

    proj_begin, proj_relay, proj_end, proj_finish = gather(
        lambda which, at, c: plane.at[part(which, at), lanes(c)], away_send, away_recv, mate_send, mate_recv
    )
    gram_begin, gram_relay, gram_end, gram_finish = gather(
        lambda which, at, c: gram.at[slim(which, at, c), pl.ds(0, (c + 1) * size)],
        gram_send, gram_recv, twin_send, twin_recv,
    )

    def share_copy(c, k, source):
        spot = shares.at[c, source, :, pl.ds(0, (c + 1) * size)]
        return remote(spot, spot, share_send.at[c, k - 1], share_recv.at[c, k - 1], line_peer(k))

    def last_block(c):
        for d in range(OUTER - 1, OUTER):
            pass_on(d, c)
            for step in (1, -1):
                source = out - step * d

                @pl.when(inside(source))
                def _(source=source):
                    add_block(source, blocks.at[source], lanes(c))
        half_copy(c).start()

    def send_parts(c):
        half_copy(c).wait_recv()
        total[half(core), lanes(c)] = total[half(core), lanes(c)] + halves[c]
        for k in range(1, nchip):
            part_copy(c, k).start()

    def sum_parts(c):
        mine = total[part(core, chip), lanes(c)]
        for k in range(1, nchip):
            part_copy(c, k).wait_recv()
            mine = mine + parts[c, k - 1]
        plane[part(core, chip), lanes(c)] = mine
        proj_begin(c)

    def send_gram(c):
        proj_end(c)
        upto = (c + 1) * size
        phi[:, lanes(c)], plo[:, lanes(c)] = split(plane[:, lanes(c)])
        some = phi[:, lanes(c)], plo[:, lanes(c)]
        work[0:size, 0:upto] = dot3(some, (phi[:, 0:upto], plo[:, 0:upto]), (((0,), (0,)), ((), ())))
        shares[c, out, :, 0:upto] = work[pl.ds(pl.multiple_of(me * thin, thin), thin), 0:upto]
        for k in range(1, OUTER):
            share_copy(c, k, out).start()

    def sum_gram(c):
        upto = (c + 1) * size
        for k in range(1, OUTER):
            share_copy(c, k, lax.rem(out + OUTER - k, OUTER)).wait_recv()
        mine = shares[c, 0, :, 0:upto]
        for k in range(1, OUTER):
            mine = mine + shares[c, k, :, 0:upto]
        gram[slim(core, chip, c), 0:upto] = mine
        gram_begin(c)

    def mirror(c):
        gram_end(c)
        for b in range(c):
            gram[b * size : (b + 1) * size, lanes(c)] = gram[lanes(c), b * size : (b + 1) * size].T

    stages = [
        (0.0, last_block), (1.1, send_parts), (4.9, sum_parts), (8.7, proj_relay), (9.7, send_gram),
        (15.6, sum_gram), (19.4, gram_relay), (20.4, mirror),
    ]
    steps = [(2.8 * c + at, c, stage) for c in range(chunks) for at, stage in stages]
    for _, c, stage in sorted(steps, key=lambda step: step[:2]):
        stage(c)

    whole = gram[...]
    scale = jnp.sqrt(jnp.sum(whole * whole, keepdims=True) + 1e-06)
    ident = (
        lax.broadcasted_iota(jnp.int32, (width, width), 0) == lax.broadcasted_iota(jnp.int32, (width, width), 1)
    ).astype(jnp.float32)
    root_scale = jnp.sqrt(scale)
    rows = root.shape[0]
    work[0:width, :] = whole / scale
    work[width : width + cols, :] = plane[pl.ds(pl.multiple_of(inn * cols, cols), cols), :]
    work[width + cols :, :] = gram[pl.ds(pl.multiple_of(col * rows, rows), rows), :] / scale

    def polar(step, carry):
        middle = split(1.5 * ident - 0.5 * work[0:width, :])
        got = dot3(split(work[...]), middle)
        work[width:, :] = got[width:, :]
        work[0:width, :] = dot3(split(got[:width, :]), middle)
        return carry

    lax.fori_loop(0, ITERS - 1, polar, 0)
    middle = split(1.5 * ident - 0.5 * work[0:width, :])
    got = dot3(split(work[width:, :]), middle)
    right[...] = got[:cols, :] / root_scale
    root[...] = got[cols:, :] * root_scale

    for step in (1, -1):
        @pl.when(both_ways(step))
        def _(step=step):
            for c in range(chunks):
                block_copy(out, step, c, True).wait_send()
    for d in range(1, OUTER):
        for step in (1, -1):
            source = out - step * d

            @pl.when(inside(source) & both_ways(step))
            def _(source=source, step=step):
                for c in range(chunks):
                    block_copy(source, step, c).wait_send()
    for d in range(OUTER):
        for k in range(1, inner):
            piece_copy(k, lax.rem(out + d, OUTER)).wait_send()
    for c in range(chunks):
        half_copy(c).wait_send()
        for k in range(1, nchip):
            part_copy(c, k).wait_send()
        for k in range(1, OUTER):
            share_copy(c, k, out).wait_send()
        proj_finish(c)
        gram_finish(c)


def solution(mesh):
    nrow, ncol = mesh.shape["row"], mesh.shape["col"]
    inner = ncol // OUTER
    nchip = nrow // 2 * inner

    def local(matrix, basis):
        cols, (depth, width) = matrix.shape[0], basis.shape
        tall = inner * cols
        size = width if LANES % (16 * nchip) else LANES
        chunks = width // size
        vmem = pl.BlockSpec(memory_space=pltpu.VMEM)

        def array(*shape, dtype=jnp.float32):
            return pltpu.VMEM(shape, dtype)

        def pair(*shape):
            return [pltpu.SemaphoreType.DMA(shape)] * 2

        root, right = pl.pallas_call(
            functools.partial(kernel, nrow, ncol, size),
            out_shape=(
                jax.ShapeDtypeStruct((width // ncol, width), jnp.float32),
                jax.ShapeDtypeStruct((cols, width), jnp.float32),
            ),
            in_specs=[pl.BlockSpec(memory_space=pltpu.HBM)] * 2,
            out_specs=(vmem, vmem),
            scratch_shapes=[
                array(OUTER, cols, depth),
                array(depth, width),
                array(OUTER, depth, width),
                array(inner - 1, OUTER, cols, depth),
                array(OUTER, tall, depth, dtype=jnp.bfloat16),
                array(OUTER, tall, depth, dtype=jnp.bfloat16),
                array(tall, width),
                array(chunks, tall // 2, size),
                array(chunks, nchip - 1, tall // (2 * nchip), size),
                array(tall, width),
                array(tall, width, dtype=jnp.bfloat16),
                array(tall, width, dtype=jnp.bfloat16),
                array(chunks, OUTER, size // (2 * nchip), width),
                array(width, width),
                array(width + cols + width // ncol, width),
                pltpu.SemaphoreType.DMA((OUTER, 2, chunks)),
                pltpu.SemaphoreType.DMA((OUTER, chunks)),
                *pair(inner - 1, OUTER),
                *pair(chunks),
                *pair(chunks, nchip - 1),
                *pair(chunks, nchip - 1),
                *pair(chunks, nchip),
                *pair(chunks, OUTER - 1),
                *pair(chunks, nchip - 1),
                *pair(chunks, nchip),
                pltpu.SemaphoreType.DMA((OUTER + 1,)),
            ],
            compiler_params=pltpu.CompilerParams(
                collective_id=0, has_side_effects=True, vmem_limit_bytes=VMEM
            ),
        )(matrix, basis)
        long = width // nrow
        part = lax.dynamic_slice(root, (0, lax.axis_index("row") * long), (width // ncol, long))
        return part.T, right

    return jax.shard_map(
        local,
        mesh=mesh,
        in_specs=(P("col", "row"), P(("row", "col"), None)),
        out_specs=(P("row", "col"), P("col", None)),
        check_vma=False,
    )
```

time: 101 us -> 85.9 us (0.85)
  Pallas kernels: 96.1 us -> 81.7 us
    pallas_call x1, Pallas kernels: 96.1 us -> 81.7 us  [local(): pl.pallas_call(functools.partial(kernel, nrow, ncol, size), out_shape=(ja...]
    unnamed x5 -> x1, local copies, waits for them, and re-layouts: 3.42 us -> 1.87 us
where the time goes in v1:
time: 85.9 us; the launch traced here: 85.6 us
  Pallas kernels  81.7 us (95%)
  local copies, waits for them, and re-layouts  3.25 us (4%)
    pallas_call x1, Pallas kernels, local(): pl.pallas_call(functools.partial(kernel, nrow, ncol, size), out_shape=(ja...  81.7 us
    unnamed x1, local copies, waits for them, and re-layouts  1.87 us

profile of v1, /device:TPU:1, one launch (start us, length us, event | category | flops | bytes accessed | tf_op | source)
XLA Modules:
  0.0 85.6 jit_solution(12458894149068806372)
XLA Ops:
  0.6 81.7 %shard_map.41 = (f32[64,512]{1,0:T(8,128)}, f32[256,512]{1,0:T(8,128)}) custom-call(f32[256,2048]{1,0:T(8,128)} %matrix.1, f32[256,512]{1,0:T(8,128)} %basis.1), custom_call_target="tpu_custom_call" | custom-call | tf_op jit(solution)/shard_map/pallas_call | solution.py:350
  82.4 1.4 %dynamic-slice_bitcast_fusion = f32[128,64]{0,1:T(8,128)} fusion(f32[64,512]{1,0:T(8,128)} %get-tuple-element.4, s32[]{:T(128)S(6)} %select_n.3), kind=kLoop, calls=%fused_computation | loop fusion | bytes 65540 | tf_op jit(solution)/shard_map/transpose | solution.py:392
  83.8 1.9 %copy.5 = f32[256,512]{1,0:T(8,128)} copy(f32[256,512]{1,0:T(8,128)} %get-tuple-element.9) | data formatting | bytes 1048576

commit v2 on v1

--- a/solution.py
+++ b/solution.py
@@ -10,7 +10,7 @@
 ITERS = 8
 OUTER = 4
 LANES = 128
-VMEM = 63 * 1024 * 1024
+VMEM = 62 * 1024 * 1024
 MESH = pl.DeviceIdType.MESH
 
 
@@ -20,9 +20,12 @@
     return hi, lo
 
 
+def dot(a, b, dims=(((1,), (0,)), ((), ()))):
+    return lax.dot_general(a, b, dimension_numbers=dims, preferred_element_type=jnp.float32)
+
+
 def dot3(a, b, dims=(((1,), (0,)), ((), ()))):
-    dot = functools.partial(lax.dot_general, dimension_numbers=dims, preferred_element_type=jnp.float32)
-    return dot(a[0], b[0]) + dot(a[0], b[1]) + dot(a[1], b[0])
+    return dot(a[0], b[0], dims) + dot(a[0], b[1], dims) + dot(a[1], b[0], dims)
 
 
 def kernel(
@@ -281,27 +284,38 @@
 
     whole = gram[...]
     scale = jnp.sqrt(jnp.sum(whole * whole, keepdims=True) + 1e-06)
-    ident = (
-        lax.broadcasted_iota(jnp.int32, (width, width), 0) == lax.broadcasted_iota(jnp.int32, (width, width), 1)
-    ).astype(jnp.float32)
     root_scale = jnp.sqrt(scale)
     rows = root.shape[0]
     work[0:width, :] = whole / scale
+    for c in range(chunks):
+        square = gram[lanes(c), lanes(c)]
+        work[lanes(c), lanes(c)] = 0.5 * (square + square.T) / scale
     work[width : width + cols, :] = plane[pl.ds(pl.multiple_of(inn * cols, cols), cols), :]
     work[width + cols :, :] = gram[pl.ds(pl.multiple_of(col * rows, rows), rows), :] / scale
 
-    def polar(step, carry):
-        middle = split(1.5 * ident - 0.5 * work[0:width, :])
-        got = dot3(split(work[...]), middle)
-        work[width:, :] = got[width:, :]
-        work[0:width, :] = dot3(split(got[:width, :]), middle)
-        return carry
-
-    lax.fori_loop(0, ITERS - 1, polar, 0)
-    middle = split(1.5 * ident - 0.5 * work[0:width, :])
-    got = dot3(split(work[width:, :]), middle)
-    right[...] = got[:cols, :] / root_scale
-    root[...] = got[cols:, :] * root_scale
+    def halves_squared(x):
+        half_product = dot(x[0], 0.5 * x[0]) + dot(x[0], x[1])
+        return half_product + half_product.T
+
+    def factor(w, w_halves):
+        e = halves_squared(w_halves) - 4.5 * w
+        return 0.0625 * halves_squared(split(e)) + (0.421875 * e - 0.5390625 * w)
+
+    for step in range(ITERS // 2):
+        w = work[0:width, :]
+        w_halves = split(w)
+        f = factor(w, w_halves)
+        f_halves = split(f)
+        rest = work[width:, :]
+        if step == ITERS // 2 - 1:
+            got = 2.25 * rest + dot3(split(rest), f_halves)
+            right[...] = got[:cols, :] / root_scale
+            root[...] = got[cols:, :] * root_scale
+        else:
+            growth = halves_squared(f_halves) + 4.5 * f
+            work[width:, :] = 2.25 * rest + dot3(split(rest), f_halves)
+            product = dot3(w_halves, split(growth))
+            work[0:width, :] = 5.0625 * w + 0.5 * (product + product.T)
 
     for step in (1, -1):
         @pl.when(both_ways(step))
@@ -350,8 +364,8 @@
         root, right = pl.pallas_call(
             functools.partial(kernel, nrow, ncol, size),
             out_shape=(
-                jax.ShapeDtypeStruct((width // ncol, width), jnp.float32),
-                jax.ShapeDtypeStruct((cols, width), jnp.float32),
+                array(width // ncol, width),
+                array(cols, width),
             ),
             in_specs=[pl.BlockSpec(memory_space=pltpu.HBM)] * 2,
             out_specs=(vmem, vmem),

time: 85.9 us -> 77.8 us (0.906)
  Pallas kernels: 81.7 us -> 75.6 us
  local copies, waits for them, and re-layouts: 3.25 us -> 1.42 us
    pallas_call x1, Pallas kernels: 81.7 us -> 75.6 us  [local(): pl.pallas_call(functools.partial(kernel, nrow, ncol, size), out_shape=(ar...]
    unnamed x1, local copies, waits for them, and re-layouts: 1.87 us -> 0.79 us
where the time goes in v2:
time: 77.8 us; the launch traced here: 77.6 us
  Pallas kernels  75.6 us (97%)
  local copies, waits for them, and re-layouts  1.42 us (2%)
    pallas_call x1, Pallas kernels, local(): pl.pallas_call(functools.partial(kernel, nrow, ncol, size), out_shape=(ar...  75.6 us

profile of v2, /device:TPU:1, one launch (start us, length us, event | category | flops | bytes accessed | tf_op | source)
XLA Modules:
  0.0 77.6 jit_solution(17959027144545939112)
XLA Ops:
  0.6 75.6 %shard_map.41 = (f32[64,512]{1,0:T(8,128)S(1)}, f32[256,512]{1,0:T(8,128)S(1)}) custom-call(f32[256,2048]{1,0:T(8,128)} %matrix.1, f32[256,512]{1,0:T(8,128)} %basis.1), custom_call_target="tpu_custom_call" | custom-call | tf_op jit(solution)/shard_map/pallas_call | solution.py:364
  76.2 0.6 dynamic-slice_bitcast_fusion
  76.8 0.8 %copy.5 = f32[256,512]{1,0:T(8,128)} copy(f32[256,512]{1,0:T(8,128)S(1)} %get-tuple-element.7) | data formatting | bytes 1048576

commit v3 on v2

--- a/solution.py
+++ b/solution.py
@@ -29,11 +29,13 @@
 
 
 def kernel(
-    nrow, ncol, size, matrix, basis, root, right,
+    nrow, ncol, size, taken, matrix, basis, root, right,
     slab, base, blocks, pieces, ahi, alo, total, halves, parts, plane, phi, plo, shares, gram, work,
+    given, lent, lent_halves, lent_parts, lent_sums, gifts,
     basis_send, basis_recv, piece_send, piece_recv, half_send, half_recv, part_send, part_recv,
     away_send, away_recv, mate_send, mate_recv, share_send, share_recv,
     gram_send, gram_recv, twin_send, twin_recv, load,
+    given_send, given_recv, lent_half_send, lent_half_recv, lent_part_send, lent_part_recv, gift_send, gift_recv,
 ):
     inner = ncol // OUTER
     nchip = nrow // 2 * inner
@@ -67,6 +69,12 @@
             src_ref=src, dst_ref=dst, send_sem=send, recv_sem=recv, device_id=device, device_id_type=MESH
         )
 
+    aside = out + 1 - 2 * lax.rem(out, 2)
+    far = OUTER - 1 - out
+    is_end = (out == 0) | (out == OUTER - 1)
+    is_middle = (out > 0) & (out < OUTER - 1)
+    aside_peer = {"row": row, "col": aside * inner + inn}
+
     def lanes(c):
         return pl.ds(c * size, size)
 
@@ -112,54 +120,98 @@
             piece_send.at[k - 1, at], piece_recv.at[k - 1, at], device,
         )
 
-    for d in range(OUTER):
+    turn = [far, out, aside, OUTER - 1 - aside]
+    for at in turn:
         for k in range(1, inner):
-            piece_copy(k, lax.rem(out + d, OUTER)).start()
+            piece_copy(k, at).start()
+
+    def given_copy(k):
+        start = pl.multiple_of((far * inner + inn) * depth, depth)
+        return remote(
+            pieces.at[k - 1, far] if k else matrix.at[:, pl.ds(start, depth)], given.at[k],
+            given_send.at[k], given_recv.at[k], aside_peer,
+        )
+
+    if taken:
+        @pl.when(is_end)
+        def _():
+            given_copy(0).start()
+
+    def home(k):
+        return pl.ds(pl.multiple_of(lax.rem(inn + inner - k, inner) * cols, cols), cols)
 
     def prepare(at, k):
         if k:
             piece_copy(k, at).wait_recv()
-        home = pl.ds(pl.multiple_of(lax.rem(inn + inner - k, inner) * cols, cols), cols)
-        ahi[at, home, :], alo[at, home, :] = split(pieces[k - 1, at] if k else slab[at])
+        ahi[at, home(k), :], alo[at, home(k), :] = split(pieces[k - 1, at] if k else slab[at])
 
     def add_block(at, block, where=slice(None), first=False):
         got = dot3((ahi[at], alo[at]), split(block[:, where]))
         total[:, where] = got if first else total[:, where] + got
 
     def pass_on(d, c):
+        goes_on = d < OUTER - 2 or c not in taken
         for step in (1, -1):
             source = out - step * d
 
             @pl.when(inside(source))
             def _(source=source, step=step):
                 block_copy(source, step, c).wait_recv()
-
-                @pl.when(both_ways(step))
-                def _():
-                    block_copy(source, step, c).start()
+                if goes_on:
+                    @pl.when(both_ways(step))
+                    def _():
+                        block_copy(source, step, c).start()
 
     for copy in loads:
         copy.wait()
     for at in range(OUTER):
         prepare(at, 0)
+
+    def add_turn(at, condition):
+        def add():
+            add_block(at, blocks.at[at])
+
+        if condition is None:
+            add()
+        else:
+            pl.when(condition)(add)
+
     for c in range(chunks):
         pass_on(1, c)
+        if c == 0:
+            for k in range(1, inner):
+                prepare(far, k)
+            if taken:
+                @pl.when(is_end)
+                def _():
+                    for k in range(1, inner):
+                        given_copy(k).start()
     for k in range(1, inner):
         prepare(out, k)
     add_block(out, base, first=True)
-    for d in range(2, OUTER - 1):
-        for c in range(chunks):
-            pass_on(d, c)
-    for d in range(1, OUTER):
+    add_turn(far, is_middle)
+    for c in range(chunks):
+        pass_on(2, c)
+        if c == chunks // 2 - 1:
+            for k in range(1, inner):
+                prepare(aside, k)
+            add_turn(aside, None)
+    if chunks == 1:
         for k in range(1, inner):
-            prepare(lax.rem(out + d, OUTER), k)
-    for d in range(1, OUTER - 1):
-        for step in (1, -1):
-            source = out - step * d
-
-            @pl.when(inside(source))
-            def _(source=source):
-                add_block(source, blocks.at[source])
+            prepare(aside, k)
+        add_turn(aside, None)
+    for k in range(1, inner):
+        prepare(OUTER - 1 - aside, k)
+    if taken:
+        @pl.when(is_middle)
+        def _():
+            for k in range(inner):
+                given_copy(k).wait_recv()
+                ahi[OUTER, home(k), :], alo[OUTER, home(k), :] = split(given[k])
+
+    def lend(n):
+        block = blocks[OUTER - 1 - aside, :, lanes(taken[n])]
+        lent[:, lanes(n)] = dot3((ahi[OUTER], alo[OUTER]), split(block))
 
     def half(which):
         return pl.ds(pl.multiple_of(which * nchip * high, nchip * high), nchip * high)
@@ -175,6 +227,38 @@
             total.at[part(core, chip_at(k)), lanes(c)], parts.at[c, k - 1],
             part_send.at[c, k - 1], part_recv.at[c, k - 1], chip_peer(k),
         )
+
+    def lent_half_copy(n):
+        return remote(
+            lent.at[half(1 - core), lanes(n)], lent_halves.at[n], lent_half_send.at[n], lent_half_recv.at[n], mate
+        )
+
+    def lent_part_copy(n, k):
+        return remote(
+            lent.at[part(core, chip_at(k)), lanes(n)], lent_parts.at[n, k - 1],
+            lent_part_send.at[n, k - 1], lent_part_recv.at[n, k - 1], chip_peer(k),
+        )
+
+    def gift_copy(n):
+        return remote(lent_sums.at[n], gifts.at[n], gift_send.at[n], gift_recv.at[n], aside_peer)
+
+    def lend_halves(n):
+        lend(n)
+        lent_half_copy(n).start()
+
+    def lend_parts(n):
+        lent_half_copy(n).wait_recv()
+        lent[half(core), lanes(n)] = lent[half(core), lanes(n)] + lent_halves[n]
+        for k in range(1, nchip):
+            lent_part_copy(n, k).start()
+
+    def give(n):
+        mine = lent[part(core, chip), lanes(n)]
+        for k in range(1, nchip):
+            lent_part_copy(n, k).wait_recv()
+            mine = mine + lent_parts[n, k - 1]
+        lent_sums[n] = mine
+        gift_copy(n).start()
 
     def gather(spot_of, send, recv, pair_send, pair_recv):
         def copy(which, at, c, send_sem, recv_sem, device):
@@ -220,20 +304,24 @@
         gram_send, gram_recv, twin_send, twin_recv,
     )
 
-    def share_copy(c, k, source):
-        spot = shares.at[c, source, :, pl.ds(0, (c + 1) * size)]
-        return remote(spot, spot, share_send.at[c, k - 1], share_recv.at[c, k - 1], line_peer(k))
+    def share(c, slot):
+        return shares.at[c, slot, :, pl.ds(0, (c + 1) * size)]
+
+    def share_copy(c):
+        return remote(share(c, 0), share(c, 1), share_send.at[c, 0], share_recv.at[c, 0], aside_peer)
+
+    def pair_copy(c, n):
+        plane_to = far if n == 0 else OUTER - 1 - aside
+        device = {"row": row, "col": plane_to * inner + inn}
+        return remote(share(c, 2), share(c, 3), share_send.at[c, 1 + n], share_recv.at[c, 1], device)
+
+    def send_half(c):
+        half_copy(c).start()
 
     def last_block(c):
-        for d in range(OUTER - 1, OUTER):
-            pass_on(d, c)
-            for step in (1, -1):
-                source = out - step * d
-
-                @pl.when(inside(source))
-                def _(source=source):
-                    add_block(source, blocks.at[source], lanes(c))
-        half_copy(c).start()
+        pass_on(OUTER - 1, c)
+        add_block(far, blocks.at[far], lanes(c))
+        send_half(c)
 
     def send_parts(c):
         half_copy(c).wait_recv()
@@ -241,11 +329,14 @@
         for k in range(1, nchip):
             part_copy(c, k).start()
 
-    def sum_parts(c):
+    def sum_parts(c, gift=None):
         mine = total[part(core, chip), lanes(c)]
         for k in range(1, nchip):
             part_copy(c, k).wait_recv()
             mine = mine + parts[c, k - 1]
+        if gift is not None:
+            gift_copy(gift).wait_recv()
+            mine = mine + gifts[gift]
         plane[part(core, chip), lanes(c)] = mine
         proj_begin(c)
 
@@ -255,18 +346,23 @@
         phi[:, lanes(c)], plo[:, lanes(c)] = split(plane[:, lanes(c)])
         some = phi[:, lanes(c)], plo[:, lanes(c)]
         work[0:size, 0:upto] = dot3(some, (phi[:, 0:upto], plo[:, 0:upto]), (((0,), (0,)), ((), ())))
-        shares[c, out, :, 0:upto] = work[pl.ds(pl.multiple_of(me * thin, thin), thin), 0:upto]
-        for k in range(1, OUTER):
-            share_copy(c, k, out).start()
+        shares[c, 0, :, 0:upto] = work[pl.ds(pl.multiple_of(me * thin, thin), thin), 0:upto]
+        share_copy(c).start()
+
+    def sum_pair(c):
+        upto = (c + 1) * size
+        share_copy(c).wait_recv()
+        shares[c, 2, :, 0:upto] = shares[c, 0, :, 0:upto] + shares[c, 1, :, 0:upto]
+
+    def send_pair(c):
+        sum_pair(c)
+        for n in range(2):
+            pair_copy(c, n).start()
 
     def sum_gram(c):
         upto = (c + 1) * size
-        for k in range(1, OUTER):
-            share_copy(c, k, lax.rem(out + OUTER - k, OUTER)).wait_recv()
-        mine = shares[c, 0, :, 0:upto]
-        for k in range(1, OUTER):
-            mine = mine + shares[c, k, :, 0:upto]
-        gram[slim(core, chip, c), 0:upto] = mine
+        pair_copy(c, 0).wait_recv()
+        gram[slim(core, chip, c), 0:upto] = shares[c, 2, :, 0:upto] + shares[c, 3, :, 0:upto]
         gram_begin(c)
 
     def mirror(c):
@@ -274,13 +370,59 @@
         for b in range(c):
             gram[b * size : (b + 1) * size, lanes(c)] = gram[lanes(c), b * size : (b + 1) * size].T
 
-    stages = [
-        (0.0, last_block), (1.1, send_parts), (4.9, sum_parts), (8.7, proj_relay), (9.7, send_gram),
-        (15.6, sum_gram), (19.4, gram_relay), (20.4, mirror),
-    ]
-    steps = [(2.8 * c + at, c, stage) for c in range(chunks) for at, stage in stages]
-    for _, c, stage in sorted(steps, key=lambda step: step[:2]):
-        stage(c)
+    def sum_with_gift(c):
+        sum_parts(c, taken.index(c))
+
+    last = OUTER - 1 - aside
+
+    def add_last(where):
+        add_block(last, blocks.at[last], where)
+
+    if chunks == 4:
+        end_order = [
+            (add_last, slice(size, 3 * size)),
+            (send_half, 1), (send_half, 2), (add_last, slice(0, size)), (add_last, slice(3 * size, width)),
+            (send_parts, 1), (send_parts, 2), (last_block, 0), (send_parts, 0),
+            (last_block, 3), (send_parts, 3), (sum_parts, 0), (sum_with_gift, 1), (sum_with_gift, 2), (sum_parts, 3),
+        ]
+        middle_order = [
+            (add_last, slice(0, 2 * size)), (send_half, 0), (send_half, 1), (lend_halves, 0), (lend_halves, 1),
+            (send_parts, 0), (add_last, slice(2 * size, width)), (send_half, 2), (send_half, 3), (lend_parts, 0), (lend_parts, 1), (send_parts, 1), (sum_parts, 0), (send_parts, 2),
+            (send_parts, 3), (give, 0), (give, 1), (sum_parts, 1), (proj_relay, 0), (sum_parts, 2), (sum_parts, 3),
+        ]
+    else:
+        lots = range(len(taken))
+        each = range(chunks)
+        end_order = [(add_last, slice(None))] + [(send_half if c in taken else last_block, c) for c in each]
+        end_order += [(send_parts, c) for c in each]
+        end_order += [(sum_with_gift if c in taken else sum_parts, c) for c in each]
+        middle_order = [(add_last, slice(None))]
+        middle_order += [(stage, n) for stage in (lend_halves, lend_parts, give) for n in lots]
+        middle_order += [(stage, c) for stage in (send_half, send_parts, sum_parts) for c in each]
+
+    for role, order in ((is_end, end_order), (is_middle, middle_order)):
+        for c in range(chunks + 2):
+            if c < chunks and (proj_relay, c) not in order:
+                order.append((proj_relay, c))
+            if 0 < c <= chunks:
+                order.append((send_gram, c - 1))
+            if c > 1 and role is is_middle:
+                order.append((send_pair, c - 2))
+        for c in range(chunks):
+            if role is is_end:
+                order.append((sum_pair, c))
+            order.append((sum_gram, c))
+
+        @pl.when(role)
+        def _(order=order):
+            for stage, c in order:
+                stage(c)
+
+    for c in range(chunks + 1):
+        if c < chunks:
+            gram_relay(c)
+        if c:
+            mirror(c - 1)
 
     whole = gram[...]
     scale = jnp.sqrt(jnp.sum(whole * whole, keepdims=True) + 1e-06)
@@ -294,28 +436,31 @@
     work[width + cols :, :] = gram[pl.ds(pl.multiple_of(col * rows, rows), rows), :] / scale
 
     def halves_squared(x):
-        half_product = dot(x[0], 0.5 * x[0]) + dot(x[0], x[1])
-        return half_product + half_product.T
-
-    def factor(w, w_halves):
-        e = halves_squared(w_halves) - 4.5 * w
-        return 0.0625 * halves_squared(split(e)) + (0.421875 * e - 0.5390625 * w)
+        cross = dot(x[0], x[1]).astype(jnp.bfloat16)
+        return dot(x[0], x[0]) + (cross.astype(jnp.float32) + cross.T.astype(jnp.float32))
 
     for step in range(ITERS // 2):
         w = work[0:width, :]
         w_halves = split(w)
-        f = factor(w, w_halves)
+        e = halves_squared(w_halves) - 4.5 * w
+        f = 0.0625 * halves_squared(split(e)) + (0.421875 * e - 0.5390625 * w)
         f_halves = split(f)
         rest = work[width:, :]
         if step == ITERS // 2 - 1:
             got = 2.25 * rest + dot3(split(rest), f_halves)
             right[...] = got[:cols, :] / root_scale
             root[...] = got[cols:, :] * root_scale
-        else:
-            growth = halves_squared(f_halves) + 4.5 * f
-            work[width:, :] = 2.25 * rest + dot3(split(rest), f_halves)
-            product = dot3(w_halves, split(growth))
-            work[0:width, :] = 5.0625 * w + 0.5 * (product + product.T)
+            break
+        growth = split(halves_squared(f_halves) + 4.5 * f)
+        work[width:, :] = 2.25 * rest + dot3(split(rest), f_halves)
+        for start in range(0, width, LANES):
+            band, after = slice(start, start + LANES), slice(start + LANES, width)
+            product = dot3([half[band] for half in w_halves], [half[:, start:] for half in growth])
+            square = product[:, :LANES]
+            work[band, band] = 5.0625 * w[band, band] + 0.5 * (square + square.T)
+            if start + LANES < width:
+                work[band, after] = 5.0625 * w[band, after] + product[:, LANES:]
+                work[after, band] = work[band, after].T
 
     for step in (1, -1):
         @pl.when(both_ways(step))
@@ -327,18 +472,38 @@
             source = out - step * d
 
             @pl.when(inside(source) & both_ways(step))
-            def _(source=source, step=step):
+            def _(source=source, step=step, d=d):
                 for c in range(chunks):
-                    block_copy(source, step, c).wait_send()
-    for d in range(OUTER):
+                    if d < OUTER - 2 or c not in taken:
+                        block_copy(source, step, c).wait_send()
+    for at in turn:
         for k in range(1, inner):
-            piece_copy(k, lax.rem(out + d, OUTER)).wait_send()
+            piece_copy(k, at).wait_send()
+    if taken:
+        @pl.when(is_end)
+        def _():
+            for k in range(inner):
+                given_copy(k).wait_send()
+
+        @pl.when(is_middle)
+        def _():
+            for n in range(len(taken)):
+                lent_half_copy(n).wait_send()
+                for k in range(1, nchip):
+                    lent_part_copy(n, k).wait_send()
+                gift_copy(n).wait_send()
+
+    @pl.when(is_middle)
+    def _():
+        for c in range(chunks):
+            for n in range(2):
+                pair_copy(c, n).wait_send()
+
     for c in range(chunks):
         half_copy(c).wait_send()
         for k in range(1, nchip):
             part_copy(c, k).wait_send()
-        for k in range(1, OUTER):
-            share_copy(c, k, out).wait_send()
+        share_copy(c).wait_send()
         proj_finish(c)
         gram_finish(c)
 
@@ -353,6 +518,8 @@
         tall = inner * cols
         size = width if LANES % (16 * nchip) else LANES
         chunks = width // size
+        taken = tuple(range(1, chunks - 1))
+        lots = max(len(taken), 1)
         vmem = pl.BlockSpec(memory_space=pltpu.VMEM)
 
         def array(*shape, dtype=jnp.float32):
@@ -362,7 +529,7 @@
             return [pltpu.SemaphoreType.DMA(shape)] * 2
 
         root, right = pl.pallas_call(
-            functools.partial(kernel, nrow, ncol, size),
+            functools.partial(kernel, nrow, ncol, size, taken),
             out_shape=(
                 array(width // ncol, width),
                 array(cols, width),
@@ -374,8 +541,8 @@
                 array(depth, width),
                 array(OUTER, depth, width),
                 array(inner - 1, OUTER, cols, depth),
-                array(OUTER, tall, depth, dtype=jnp.bfloat16),
-                array(OUTER, tall, depth, dtype=jnp.bfloat16),
+                array(OUTER + 1, tall, depth, dtype=jnp.bfloat16),
+                array(OUTER + 1, tall, depth, dtype=jnp.bfloat16),
                 array(tall, width),
                 array(chunks, tall // 2, size),
                 array(chunks, nchip - 1, tall // (2 * nchip), size),
@@ -385,6 +552,12 @@
                 array(chunks, OUTER, size // (2 * nchip), width),
                 array(width, width),
                 array(width + cols + width // ncol, width),
+                array(inner, cols, depth),
+                array(tall, lots * size),
+                array(lots, tall // 2, size),
+                array(lots, nchip - 1, tall // (2 * nchip), size),
+                array(lots, tall // (2 * nchip), size),
+                array(lots, tall // (2 * nchip), size),
                 pltpu.SemaphoreType.DMA((OUTER, 2, chunks)),
                 pltpu.SemaphoreType.DMA((OUTER, chunks)),
                 *pair(inner - 1, OUTER),
@@ -396,6 +569,10 @@
                 *pair(chunks, nchip - 1),
                 *pair(chunks, nchip),
                 pltpu.SemaphoreType.DMA((OUTER + 1,)),
+                *pair(inner),
+                *pair(lots),
+                *pair(lots, nchip - 1),
+                *pair(lots),
             ],
             compiler_params=pltpu.CompilerParams(
                 collective_id=0, has_side_effects=True, vmem_limit_bytes=VMEM

time: 77.8 us -> 75.9 us (0.976)
  Pallas kernels: 75.6 us -> 73.7 us
    pallas_call x1, Pallas kernels: 75.6 us -> 73.7 us  [local(): pl.pallas_call(functools.partial(kernel, nrow, ncol, size, taken), out_sh...]
where the time goes in v3:
time: 75.9 us; the launch traced here: 75.7 us
  Pallas kernels  73.7 us (97%)
  local copies, waits for them, and re-layouts  1.42 us (2%)
    pallas_call x1, Pallas kernels, local(): pl.pallas_call(functools.partial(kernel, nrow, ncol, size, taken), out_sh...  73.7 us

profile of v3, /device:TPU:1, one launch (start us, length us, event | category | flops | bytes accessed | tf_op | source)
XLA Modules:
  0.0 75.7 jit_solution(9236417419109568915)
XLA Ops:
  0.6 73.7 %shard_map.41 = (f32[64,512]{1,0:T(8,128)S(1)}, f32[256,512]{1,0:T(8,128)S(1)}) custom-call(f32[256,2048]{1,0:T(8,128)} %matrix.1, f32[256,512]{1,0:T(8,128)} %basis.1), custom_call_target="tpu_custom_call" | custom-call | tf_op jit(solution)/shard_map/pallas_call | solution.py:531
  74.3 0.6 dynamic-slice_bitcast_fusion
  74.9 0.8 %copy.5 = f32[256,512]{1,0:T(8,128)} copy(f32[256,512]{1,0:T(8,128)S(1)} %get-tuple-element.7) | data formatting | bytes 1048576

commit v4 on v3

--- a/solution.py
+++ b/solution.py
@@ -30,12 +30,13 @@
 
 def kernel(
     nrow, ncol, size, taken, matrix, basis, root, right,
-    slab, base, blocks, pieces, ahi, alo, total, halves, parts, plane, phi, plo, shares, gram, work,
+    slab, base, blocks, pieces, ahi, alo, total, halves, parts, plane, phi, plo, strip, strip_halves, strip_parts, shares, gram, work,
     given, lent, lent_halves, lent_parts, lent_sums, gifts,
     basis_send, basis_recv, piece_send, piece_recv, half_send, half_recv, part_send, part_recv,
     away_send, away_recv, mate_send, mate_recv, share_send, share_recv,
     gram_send, gram_recv, twin_send, twin_recv, load,
     given_send, given_recv, lent_half_send, lent_half_recv, lent_part_send, lent_part_recv, gift_send, gift_recv,
+    strip_half_send, strip_half_recv, strip_part_send, strip_part_recv,
 ):
     inner = ncol // OUTER
     nchip = nrow // 2 * inner
@@ -260,7 +261,7 @@
         lent_sums[n] = mine
         gift_copy(n).start()
 
-    def gather(spot_of, send, recv, pair_send, pair_recv):
+    def gather(spot_of, send, recv, pair_send, pair_recv, wanted=None):
         def copy(which, at, c, send_sem, recv_sem, device):
             spot = spot_of(which, at, c)
             return remote(spot, spot, send_sem, recv_sem, device)
@@ -271,33 +272,54 @@
         def across(c, k, which):
             return copy(which, from_chip(k), c, pair_send.at[c, k], pair_recv.at[c, k], mate)
 
+        def when(which, at, target):
+            if wanted is None:
+                return lambda act: act()
+            return pl.when(wanted(which, at, lax.rem(target, inner)))
+
         def begin(c):
             for k in range(1, nchip):
-                away(c, k, chip).start()
-            across(c, 0, core).start()
+                @when(core, chip, chip_at(k))
+                def _(k=k):
+                    away(c, k, chip).start()
+
+            @when(core, chip, chip)
+            def _():
+                across(c, 0, core).start()
 
         def relay(c):
             for k in range(1, nchip):
-                away(c, k, from_chip(k)).wait_recv()
-                across(c, k, core).start()
+                @when(core, from_chip(k), chip)
+                def _(k=k):
+                    away(c, k, from_chip(k)).wait_recv()
+                    across(c, k, core).start()
 
         def end(c):
             for k in range(nchip):
-                across(c, k, 1 - core).wait_recv()
+                @when(1 - core, from_chip(k), chip)
+                def _(k=k):
+                    across(c, k, 1 - core).wait_recv()
 
         def finish(c):
             for k in range(1, nchip):
-                away(c, k, chip).wait_send()
+                @when(core, chip, chip_at(k))
+                def _(k=k):
+                    away(c, k, chip).wait_send()
             for k in range(nchip):
-                across(c, k, core).wait_send()
+                @when(core, from_chip(k), chip)
+                def _(k=k):
+                    across(c, k, core).wait_send()
 
         return begin, relay, end, finish
+
+    def columns_of(which, at, inner_at):
+        return (which * nchip + at) * high // cols == inner_at
 
     def slim(which, at, c):
         return pl.ds(pl.multiple_of(c * size + (which * nchip + at) * thin, thin), thin)
 
     proj_begin, proj_relay, proj_end, proj_finish = gather(
-        lambda which, at, c: plane.at[part(which, at), lanes(c)], away_send, away_recv, mate_send, mate_recv
+        lambda which, at, c: plane.at[part(which, at), lanes(c)], away_send, away_recv, mate_send, mate_recv, columns_of
     )
     gram_begin, gram_relay, gram_end, gram_finish = gather(
         lambda which, at, c: gram.at[slim(which, at, c), pl.ds(0, (c + 1) * size)],
@@ -338,15 +360,49 @@
             gift_copy(gift).wait_recv()
             mine = mine + gifts[gift]
         plane[part(core, chip), lanes(c)] = mine
-        proj_begin(c)
+        local_gram(c, mine)
+
+    def strip_half(which):
+        return pl.ds(pl.multiple_of(which * nchip * thin, nchip * thin), nchip * thin)
+
+    def strip_band(which, at):
+        return pl.ds(pl.multiple_of((which * nchip + at) * thin, thin), thin)
+
+    def strip_half_copy(c):
+        wide = pl.ds(0, (c + 1) * size)
+        return remote(
+            strip.at[c, strip_half(1 - core), wide], strip_halves.at[c, :, wide],
+            strip_half_send.at[c], strip_half_recv.at[c], mate,
+        )
+
+    def strip_part_copy(c, k):
+        wide = pl.ds(0, (c + 1) * size)
+        return remote(
+            strip.at[c, strip_band(core, chip_at(k)), wide], strip_parts.at[c, k - 1, :, wide],
+            strip_part_send.at[c, k - 1], strip_part_recv.at[c, k - 1], chip_peer(k),
+        )
+
+    def local_gram(c, mine):
+        upto = (c + 1) * size
+        some = split(mine)
+        phi[:, lanes(c)], plo[:, lanes(c)] = some
+        strip[c, :, 0:upto] = dot3(some, (phi[:, 0:upto], plo[:, 0:upto]), (((0,), (0,)), ((), ())))
+        strip_half_copy(c).start()
+
+    def send_strips(c):
+        upto = (c + 1) * size
+        strip_half_copy(c).wait_recv()
+        strip[c, strip_half(core), 0:upto] = strip[c, strip_half(core), 0:upto] + strip_halves[c, :, 0:upto]
+        for k in range(1, nchip):
+            strip_part_copy(c, k).start()
 
     def send_gram(c):
-        proj_end(c)
         upto = (c + 1) * size
-        phi[:, lanes(c)], plo[:, lanes(c)] = split(plane[:, lanes(c)])
-        some = phi[:, lanes(c)], plo[:, lanes(c)]
-        work[0:size, 0:upto] = dot3(some, (phi[:, 0:upto], plo[:, 0:upto]), (((0,), (0,)), ((), ())))
-        shares[c, 0, :, 0:upto] = work[pl.ds(pl.multiple_of(me * thin, thin), thin), 0:upto]
+        mine = strip[c, strip_band(core, chip), 0:upto]
+        for k in range(1, nchip):
+            strip_part_copy(c, k).wait_recv()
+            mine = mine + strip_parts[c, k - 1, :, 0:upto]
+        shares[c, 0, :, 0:upto] = mine
         share_copy(c).start()
 
     def sum_pair(c):
@@ -365,10 +421,19 @@
         gram[slim(core, chip, c), 0:upto] = shares[c, 2, :, 0:upto] + shares[c, 3, :, 0:upto]
         gram_begin(c)
 
+    squares = []
+
     def mirror(c):
         gram_end(c)
+        square = gram[lanes(c), lanes(c)]
+        square = 0.5 * (square + square.T)
+        work[lanes(c), lanes(c)] = square
+        squares.append(jnp.sum(square * square, keepdims=True))
         for b in range(c):
-            gram[b * size : (b + 1) * size, lanes(c)] = gram[lanes(c), b * size : (b + 1) * size].T
+            block = gram[lanes(c), lanes(b)]
+            work[lanes(c), lanes(b)] = block
+            work[lanes(b), lanes(c)] = block.T
+            squares.append(2.0 * jnp.sum(block * block, keepdims=True))
 
     def sum_with_gift(c):
         sum_parts(c, taken.index(c))
@@ -383,12 +448,15 @@
             (add_last, slice(size, 3 * size)),
             (send_half, 1), (send_half, 2), (add_last, slice(0, size)), (add_last, slice(3 * size, width)),
             (send_parts, 1), (send_parts, 2), (last_block, 0), (send_parts, 0),
-            (last_block, 3), (send_parts, 3), (sum_parts, 0), (sum_with_gift, 1), (sum_with_gift, 2), (sum_parts, 3),
+            (last_block, 3), (send_parts, 3), (sum_parts, 0), (sum_with_gift, 1), (send_strips, 0),
+            (sum_with_gift, 2), (send_strips, 1), (sum_parts, 3), (send_strips, 2), (send_strips, 3),
         ]
         middle_order = [
             (add_last, slice(0, 2 * size)), (send_half, 0), (send_half, 1), (lend_halves, 0), (lend_halves, 1),
-            (send_parts, 0), (add_last, slice(2 * size, width)), (send_half, 2), (send_half, 3), (lend_parts, 0), (lend_parts, 1), (send_parts, 1), (sum_parts, 0), (send_parts, 2),
-            (send_parts, 3), (give, 0), (give, 1), (sum_parts, 1), (proj_relay, 0), (sum_parts, 2), (sum_parts, 3),
+            (send_parts, 0), (add_last, slice(2 * size, width)), (send_half, 2), (send_half, 3), (lend_parts, 0),
+            (lend_parts, 1), (send_parts, 1), (send_parts, 2), (send_parts, 3), (sum_parts, 0),
+            (give, 0), (give, 1), (send_strips, 0), (sum_parts, 1), (sum_parts, 2), (send_strips, 1),
+            (sum_parts, 3), (send_strips, 2), (send_strips, 3),
         ]
     else:
         lots = range(len(taken))
@@ -396,18 +464,18 @@
         end_order = [(add_last, slice(None))] + [(send_half if c in taken else last_block, c) for c in each]
         end_order += [(send_parts, c) for c in each]
         end_order += [(sum_with_gift if c in taken else sum_parts, c) for c in each]
+        end_order += [(send_strips, c) for c in each]
         middle_order = [(add_last, slice(None))]
         middle_order += [(stage, n) for stage in (lend_halves, lend_parts, give) for n in lots]
-        middle_order += [(stage, c) for stage in (send_half, send_parts, sum_parts) for c in each]
+        middle_order += [(stage, c) for stage in (send_half, send_parts, sum_parts, send_strips) for c in each]
 
     for role, order in ((is_end, end_order), (is_middle, middle_order)):
-        for c in range(chunks + 2):
-            if c < chunks and (proj_relay, c) not in order:
-                order.append((proj_relay, c))
-            if 0 < c <= chunks:
-                order.append((send_gram, c - 1))
-            if c > 1 and role is is_middle:
-                order.append((send_pair, c - 2))
+        order += [(proj_begin, c) for c in range(chunks)]
+        for c in range(chunks + 1):
+            if c < chunks:
+                order.append((send_gram, c))
+            if c and role is is_middle:
+                order.append((send_pair, c - 1))
         for c in range(chunks):
             if role is is_end:
                 order.append((sum_pair, c))
@@ -421,19 +489,16 @@
     for c in range(chunks + 1):
         if c < chunks:
             gram_relay(c)
+        if c == chunks - 1:
+            for past in range(chunks):
+                proj_relay(past)
         if c:
             mirror(c - 1)
 
-    whole = gram[...]
-    scale = jnp.sqrt(jnp.sum(whole * whole, keepdims=True) + 1e-06)
+    scale = jnp.sqrt(sum(squares) + 1e-06)
     root_scale = jnp.sqrt(scale)
+    per_scale = 1.0 / scale
     rows = root.shape[0]
-    work[0:width, :] = whole / scale
-    for c in range(chunks):
-        square = gram[lanes(c), lanes(c)]
-        work[lanes(c), lanes(c)] = 0.5 * (square + square.T) / scale
-    work[width : width + cols, :] = plane[pl.ds(pl.multiple_of(inn * cols, cols), cols), :]
-    work[width + cols :, :] = gram[pl.ds(pl.multiple_of(col * rows, rows), rows), :] / scale
 
     def halves_squared(x):
         cross = dot(x[0], x[1]).astype(jnp.bfloat16)
@@ -442,20 +507,32 @@
     for step in range(ITERS // 2):
         w = work[0:width, :]
         w_halves = split(w)
-        e = halves_squared(w_halves) - 4.5 * w
+        e = halves_squared(w_halves)
+        if step == 0:
+            w = w * per_scale
+            e = e * (per_scale * per_scale)
+        e = e - 4.5 * w
         f = 0.0625 * halves_squared(split(e)) + (0.421875 * e - 0.5390625 * w)
         f_halves = split(f)
-        rest = work[width:, :]
         if step == ITERS // 2 - 1:
+            rest = work[width:, :]
             got = 2.25 * rest + dot3(split(rest), f_halves)
             right[...] = got[:cols, :] / root_scale
             root[...] = got[cols:, :] * root_scale
             break
         growth = split(halves_squared(f_halves) + 4.5 * f)
+        if step == 0:
+            for c in range(chunks):
+                proj_end(c)
+            work[width : width + cols, :] = plane[pl.ds(pl.multiple_of(inn * cols, cols), cols), :]
+            work[width + cols :, :] = work[pl.ds(pl.multiple_of(col * rows, rows), rows), :] * per_scale
+        rest = work[width:, :]
         work[width:, :] = 2.25 * rest + dot3(split(rest), f_halves)
         for start in range(0, width, LANES):
             band, after = slice(start, start + LANES), slice(start + LANES, width)
             product = dot3([half[band] for half in w_halves], [half[:, start:] for half in growth])
+            if step == 0:
+                product = product * per_scale
             square = product[:, :LANES]
             work[band, band] = 5.0625 * w[band, band] + 0.5 * (square + square.T)
             if start + LANES < width:
@@ -504,6 +581,9 @@
         for k in range(1, nchip):
             part_copy(c, k).wait_send()
         share_copy(c).wait_send()
+        strip_half_copy(c).wait_send()
+        for k in range(1, nchip):
+            strip_part_copy(c, k).wait_send()
         proj_finish(c)
         gram_finish(c)
 
@@ -547,8 +627,11 @@
                 array(chunks, tall // 2, size),
                 array(chunks, nchip - 1, tall // (2 * nchip), size),
                 array(tall, width),
-                array(tall, width, dtype=jnp.bfloat16),
-                array(tall, width, dtype=jnp.bfloat16),
+                array(tall // (2 * nchip), width, dtype=jnp.bfloat16),
+                array(tall // (2 * nchip), width, dtype=jnp.bfloat16),
+                array(chunks, size, width),
+                array(chunks, size // 2, width),
+                array(chunks, nchip - 1, size // (2 * nchip), width),
                 array(chunks, OUTER, size // (2 * nchip), width),
                 array(width, width),
                 array(width + cols + width // ncol, width),
@@ -573,6 +656,8 @@
                 *pair(lots),
                 *pair(lots, nchip - 1),
                 *pair(lots),
+                *pair(chunks),
+                *pair(chunks, nchip - 1),
             ],
             compiler_params=pltpu.CompilerParams(
                 collective_id=0, has_side_effects=True, vmem_limit_bytes=VMEM

time: 75.9 us -> 74.7 us (0.984)
  Pallas kernels: 73.7 us -> 72.5 us
    pallas_call x1, Pallas kernels: 73.7 us -> 72.5 us  [local(): pl.pallas_call(functools.partial(kernel, nrow, ncol, size, taken), out_sh...]
where the time goes in v4:
time: 74.7 us; the launch traced here: 74.6 us
  Pallas kernels  72.5 us (97%)
  local copies, waits for them, and re-layouts  1.42 us (2%)
    pallas_call x1, Pallas kernels, local(): pl.pallas_call(functools.partial(kernel, nrow, ncol, size, taken), out_sh...  72.5 us

profile of v4, /device:TPU:1, one launch (start us, length us, event | category | flops | bytes accessed | tf_op | source)
XLA Modules:
  0.0 74.6 jit_solution(7642355105827315919)
XLA Ops:
  0.6 72.5 %shard_map.41 = (f32[64,512]{1,0:T(8,128)S(1)}, f32[256,512]{1,0:T(8,128)S(1)}) custom-call(f32[256,2048]{1,0:T(8,128)} %matrix.1, f32[256,512]{1,0:T(8,128)} %basis.1), custom_call_target="tpu_custom_call" | custom-call | tf_op jit(solution)/shard_map/pallas_call | solution.py:611
  73.1 0.6 dynamic-slice_bitcast_fusion
  73.8 0.8 %copy.5 = f32[256,512]{1,0:T(8,128)} copy(f32[256,512]{1,0:T(8,128)S(1)} %get-tuple-element.7) | data formatting | bytes 1048576

commit v5 on v4

--- a/solution.py
+++ b/solution.py
@@ -452,8 +452,8 @@
             (sum_with_gift, 2), (send_strips, 1), (sum_parts, 3), (send_strips, 2), (send_strips, 3),
         ]
         middle_order = [
-            (add_last, slice(0, 2 * size)), (send_half, 0), (send_half, 1), (lend_halves, 0), (lend_halves, 1),
-            (send_parts, 0), (add_last, slice(2 * size, width)), (send_half, 2), (send_half, 3), (lend_parts, 0),
+            (add_last, slice(0, size)), (send_half, 0), (lend_halves, 0), (lend_halves, 1), (send_parts, 0),
+            (add_last, slice(size, width)), (send_half, 1), (send_half, 2), (send_half, 3), (lend_parts, 0),
             (lend_parts, 1), (send_parts, 1), (send_parts, 2), (send_parts, 3), (sum_parts, 0),
             (give, 0), (give, 1), (send_strips, 0), (sum_parts, 1), (sum_parts, 2), (send_strips, 1),
             (sum_parts, 3), (send_strips, 2), (send_strips, 3),
@@ -486,6 +486,52 @@
             for stage, c in order:
                 stage(c)
 
+    for step in (1, -1):
+        @pl.when(both_ways(step))
+        def _(step=step):
+            for c in range(chunks):
+                block_copy(out, step, c, True).wait_send()
+    for d in range(1, OUTER):
+        for step in (1, -1):
+            source = out - step * d
+
+            @pl.when(inside(source) & both_ways(step))
+            def _(source=source, step=step, d=d):
+                for c in range(chunks):
+                    if d < OUTER - 2 or c not in taken:
+                        block_copy(source, step, c).wait_send()
+    for at in turn:
+        for k in range(1, inner):
+            piece_copy(k, at).wait_send()
+    if taken:
+        @pl.when(is_end)
+        def _():
+            for k in range(inner):
+                given_copy(k).wait_send()
+
+        @pl.when(is_middle)
+        def _():
+            for n in range(len(taken)):
+                lent_half_copy(n).wait_send()
+                for k in range(1, nchip):
+                    lent_part_copy(n, k).wait_send()
+                gift_copy(n).wait_send()
+
+    @pl.when(is_middle)
+    def _():
+        for c in range(chunks):
+            for n in range(2):
+                pair_copy(c, n).wait_send()
+
+    for c in range(chunks):
+        half_copy(c).wait_send()
+        for k in range(1, nchip):
+            part_copy(c, k).wait_send()
+        share_copy(c).wait_send()
+        strip_half_copy(c).wait_send()
+        for k in range(1, nchip):
+            strip_part_copy(c, k).wait_send()
+
     for c in range(chunks + 1):
         if c < chunks:
             gram_relay(c)
@@ -517,8 +563,13 @@
         if step == ITERS // 2 - 1:
             rest = work[width:, :]
             got = 2.25 * rest + dot3(split(rest), f_halves)
-            right[...] = got[:cols, :] / root_scale
-            root[...] = got[cols:, :] * root_scale
+            right[...] = got[:cols, :] * (1.0 / root_scale)
+            if root.shape[1] == width:
+                root[...] = got[cols:, :] * root_scale
+            else:
+                work[width + cols :, :] = got[cols:, :]
+                long = root.shape[1]
+                root[...] = work[width + cols :, pl.ds(pl.multiple_of(row * long, long), long)] * root_scale
             break
         growth = split(halves_squared(f_halves) + 4.5 * f)
         if step == 0:
@@ -539,51 +590,7 @@
                 work[band, after] = 5.0625 * w[band, after] + product[:, LANES:]
                 work[after, band] = work[band, after].T
 
-    for step in (1, -1):
-        @pl.when(both_ways(step))
-        def _(step=step):
-            for c in range(chunks):
-                block_copy(out, step, c, True).wait_send()
-    for d in range(1, OUTER):
-        for step in (1, -1):
-            source = out - step * d
-
-            @pl.when(inside(source) & both_ways(step))
-            def _(source=source, step=step, d=d):
-                for c in range(chunks):
-                    if d < OUTER - 2 or c not in taken:
-                        block_copy(source, step, c).wait_send()
-    for at in turn:
-        for k in range(1, inner):
-            piece_copy(k, at).wait_send()
-    if taken:
-        @pl.when(is_end)
-        def _():
-            for k in range(inner):
-                given_copy(k).wait_send()
-
-        @pl.when(is_middle)
-        def _():
-            for n in range(len(taken)):
-                lent_half_copy(n).wait_send()
-                for k in range(1, nchip):
-                    lent_part_copy(n, k).wait_send()
-                gift_copy(n).wait_send()
-
-    @pl.when(is_middle)
-    def _():
-        for c in range(chunks):
-            for n in range(2):
-                pair_copy(c, n).wait_send()
-
     for c in range(chunks):
-        half_copy(c).wait_send()
-        for k in range(1, nchip):
-            part_copy(c, k).wait_send()
-        share_copy(c).wait_send()
-        strip_half_copy(c).wait_send()
-        for k in range(1, nchip):
-            strip_part_copy(c, k).wait_send()
         proj_finish(c)
         gram_finish(c)
 
@@ -608,10 +615,11 @@
         def pair(*shape):
             return [pltpu.SemaphoreType.DMA(shape)] * 2
 
+        long = width // nrow
         root, right = pl.pallas_call(
             functools.partial(kernel, nrow, ncol, size, taken),
             out_shape=(
-                array(width // ncol, width),
+                array(width // ncol, width if long % LANES else long),
                 array(cols, width),
             ),
             in_specs=[pl.BlockSpec(memory_space=pltpu.HBM)] * 2,
@@ -663,7 +671,8 @@
                 collective_id=0, has_side_effects=True, vmem_limit_bytes=VMEM
             ),
         )(matrix, basis)
-        long = width // nrow
+        if long % LANES == 0:
+            return root.T, right
         part = lax.dynamic_slice(root, (0, lax.axis_index("row") * long), (width // ncol, long))
         return part.T, right
 

time: 74.7 us -> 74.5 us (level)
  no operation moved by 1% of the time
where the time goes in v5:
time: 74.5 us; the launch traced here: 74.3 us
  Pallas kernels  72.3 us (97%)
  local copies, waits for them, and re-layouts  1.41 us (2%)
    pallas_call x1, Pallas kernels, local(): pl.pallas_call(functools.partial(kernel, nrow, ncol, size, taken), out_sh...  72.3 us

profile of v5, /device:TPU:1, one launch (start us, length us, event | category | flops | bytes accessed | tf_op | source)
XLA Modules:
  0.0 74.3 jit_solution(9282547671404952271)
XLA Ops:
  0.6 72.3 %shard_map.41 = (f32[64,128]{1,0:T(8,128)S(1)}, f32[256,512]{1,0:T(8,128)S(1)}) custom-call(f32[256,2048]{1,0:T(8,128)} %matrix.1, f32[256,512]{1,0:T(8,128)} %basis.1), custom_call_target="tpu_custom_call" | custom-call | tf_op jit(solution)/shard_map/pallas_call | solution.py:619
  72.9 0.6 copy.6
  73.5 0.8 %copy.7 = f32[256,512]{1,0:T(8,128)} copy(f32[256,512]{1,0:T(8,128)S(1)} %get-tuple-element.7) | data formatting | bytes 1048576

commit v6 on v5

--- a/solution.py
+++ b/solution.py
@@ -428,12 +428,12 @@
         square = gram[lanes(c), lanes(c)]
         square = 0.5 * (square + square.T)
         work[lanes(c), lanes(c)] = square
-        squares.append(jnp.sum(square * square, keepdims=True))
+        squares.append(square * square)
         for b in range(c):
             block = gram[lanes(c), lanes(b)]
             work[lanes(c), lanes(b)] = block
             work[lanes(b), lanes(c)] = block.T
-            squares.append(2.0 * jnp.sum(block * block, keepdims=True))
+            squares.append(2.0 * (block * block))
 
     def sum_with_gift(c):
         sum_parts(c, taken.index(c))
@@ -541,7 +541,7 @@
         if c:
             mirror(c - 1)
 
-    scale = jnp.sqrt(sum(squares) + 1e-06)
+    scale = jnp.sqrt(jnp.sum(sum(squares[1:], squares[0]), keepdims=True) + 1e-06)
     root_scale = jnp.sqrt(scale)
     per_scale = 1.0 / scale
     rows = root.shape[0]

time: 74.5 us -> 74.5 us (level)
  no operation moved by 1% of the time
where the time goes in v6:
time: 74.5 us; the launch traced here: 74.3 us
  Pallas kernels  72.3 us (97%)
  local copies, waits for them, and re-layouts  1.41 us (2%)
    pallas_call x1, Pallas kernels, local(): pl.pallas_call(functools.partial(kernel, nrow, ncol, size, taken), out_sh...  72.3 us

profile of v6, /device:TPU:1, one launch (start us, length us, event | category | flops | bytes accessed | tf_op | source)
XLA Modules:
  0.0 74.3 jit_solution(6544999047076047288)
XLA Ops:
  0.6 72.3 %shard_map.41 = (f32[64,128]{1,0:T(8,128)S(1)}, f32[256,512]{1,0:T(8,128)S(1)}) custom-call(f32[256,2048]{1,0:T(8,128)} %matrix.1, f32[256,512]{1,0:T(8,128)} %basis.1), custom_call_target="tpu_custom_call" | custom-call | tf_op jit(solution)/shard_map/pallas_call | solution.py:619
  72.9 0.6 copy.6
  73.5 0.8 %copy.7 = f32[256,512]{1,0:T(8,128)} copy(f32[256,512]{1,0:T(8,128)S(1)} %get-tuple-element.7) | data formatting | bytes 1048576
